TPU v7x, 32 devices: a whole 2x2x4 slice. The times are simulated.
32 devices in a mesh: groups: 2 (over y), users: 4 (over z), routers: 2 (over x), heads: 2 (over core).
Axes of the slice: x: 2, y: 2, z: 4, core: 2. Of those that a mesh axis runs over, the one named last changes fastest.
Arguments:
- items: bfloat16 [64, 64, 1024], P(('groups', 'users', 'routers')), parts along dimension 0, may hold values from -6 to 6
- block_owner: int32 [64, 1], P(('groups', 'users', 'routers')), parts along dimension 0, may hold values from 0 to 3; in each aligned block of 4 rows (0 to 3, 4 to 7, ...) at most 2 rows name the same one
- block_user: int32 [64], P(('groups', 'users', 'routers')), parts along dimension 0, may hold values from 0 to 1
- block_fill: int32 [64], P(('groups', 'users', 'routers')), parts along dimension 0, may hold values from 1 to 64
- prefix_keys: bfloat16 [16, 256, 1024], P(('groups', 'users'), None, 'heads'), parts along dimension 0, may hold values from -6 to 6
- prefix_values: bfloat16 [16, 256, 1024], P(('groups', 'users'), None, 'heads'), parts along dimension 0, may hold values from -6 to 6
- w_in: bfloat16 [4, 1024, 1024], P(None, 'routers', 'heads'), may hold values from -0.1875 to 0.1875
- attn_gain: bfloat16 [1024], P('heads'), may hold values from 0.25 to 1.75
- w_o: bfloat16 [1024, 1024], P('heads', 'routers'), may hold values from -0.1875 to 0.1875
- mlp_gain: bfloat16 [1024], replicated, may hold values from 0.25 to 1.75
- w_one: bfloat16 [1024, 256], replicated, may hold values from -0.1875 to 0.1875
- w_two: bfloat16 [256], replicated, may hold values from -0.375 to 0.375
Outputs:
- scores: float32 [64, 64], P(('groups', 'users', 'routers')), parts along dimension 0
There are 2 independent parts, one for each index of `groups`. A program takes and returns all parts, laid end to end along the dimension named above; an argument that names none is the same for every part. Nothing has to cross between parts.
Inputs may be any that keep to these rules, and one draw needn't show every extreme that they name: `block_owner`: within the rows of one device (aligned blocks of 4 blocks), no owner is named by more than 2 rows, and in every draw some owner is named by exactly 2 rows of some device.
All inputs are finite; a program needn't handle non-finite values.
Results may differ from a plain program's by a relative error of at most 0.005.
Values may be sent and summed in bfloat16 or wider, within the bound.
A program may use at most 64 MiB of HBM per device.

v0:
```python
import jax
import jax.numpy as jnp
from jax import lax
from jax.sharding import PartitionSpec as P

D = 1024
HEAD_DIM = 128
CAP = 2
HD = 1024
EPSILON = 1e-05


def prefix_attention(group_queries, group_users, prefix_keys, prefix_values):
    group_size, block_width, half_width = group_queries.shape
    heads_here = half_width // HEAD_DIM
    safe_user = jnp.maximum(group_users, 0)
    user_keys = jnp.take(prefix_keys, safe_user, axis=0)
    user_values = jnp.take(prefix_values, safe_user, axis=0)
    query_heads = group_queries.reshape(group_size, block_width, heads_here, HEAD_DIM)
    key_heads = user_keys.reshape(group_size, -1, heads_here, HEAD_DIM)
    value_heads = user_values.reshape(group_size, -1, heads_here, HEAD_DIM)
    raw_scores = jnp.einsum(
        "gqhd,gkhd->ghqk", query_heads, key_heads, preferred_element_type=jnp.float32
    ) * HEAD_DIM ** (-0.5)
    weights = jax.nn.silu(raw_scores).astype(jnp.bfloat16)
    summed = jnp.einsum("ghqk,gkhd->gqhd", weights, value_heads, preferred_element_type=jnp.float32)
    return summed.reshape(group_size, block_width, half_width).astype(jnp.bfloat16)


def local(
    items,
    block_owner,
    block_user,
    block_fill,
    prefix_keys,
    prefix_values,
    w_in,
    attn_gain,
    w_o,
    mlp_gain,
    w_one,
    w_two,
):
    blocks, block_width, model_width = items.shape
    row_count = blocks * block_width
    half_width = w_in.shape[2]
    heads_here = half_width // HEAD_DIM
    peer_count = lax.axis_size("users")
    slot_count = peer_count * CAP
    score_scale = HEAD_DIM ** (-0.5)
    flat_items = items.reshape(row_count, model_width)
    projected = jnp.einsum(
        "rk,pkc->prc",
        flat_items,
        lax.all_gather(w_in, "routers", axis=1, tiled=True),
        preferred_element_type=jnp.float32,
    )
    activated = jax.nn.silu(projected)
    queries = activated[0].astype(jnp.bfloat16)
    target = block_owner[:, 0]
    earlier = lax.broadcasted_iota(jnp.int32, (blocks, blocks), 1) < lax.broadcasted_iota(
        jnp.int32, (blocks, blocks), 0
    )
    same_target = target[:, None] == target[None, :]
    dest_rank = jnp.sum((same_target & earlier).astype(jnp.int32), axis=1)
    position = target * CAP + dest_rank
    selector = lax.broadcasted_iota(jnp.int32, (slot_count, blocks), 0) == position[None, :]
    block_queries = queries.reshape(blocks, block_width * half_width)
    outgoing = jnp.dot(
        selector.astype(jnp.bfloat16), block_queries, preferred_element_type=jnp.float32
    ).astype(jnp.bfloat16)
    outgoing = outgoing.reshape(peer_count, CAP, block_width, half_width)
    slot_user = jnp.sum(jnp.where(selector, block_user[None, :] + 1, 0), axis=1) - 1
    slot_user = slot_user.reshape(peer_count, CAP)
    arrived = lax.all_to_all(outgoing, "users", split_axis=0, concat_axis=0, tiled=True)
    arrived_users = lax.all_to_all(slot_user, "users", split_axis=0, concat_axis=0, tiled=True)
    sources, per_source = arrived_users.shape
    total_slots = sources * per_source
    flat_queries = arrived.reshape(total_slots, block_width, half_width)
    flat_users = arrived_users.reshape(total_slots)
    packing = jnp.argsort((flat_users < 0).astype(jnp.int32), stable=True)
    used_slots = jnp.sum((flat_users >= 0).astype(jnp.int32))
    packed_queries = jnp.take(flat_queries, packing, axis=0)
    packed_users = jnp.take(flat_users, packing, axis=0)
    needed = (used_slots + 3) // 4

    def attend_group(group_index, buffer):
        first_slot = group_index * 4
        group_queries = lax.dynamic_slice_in_dim(packed_queries, first_slot, 4, 0)
        group_users = lax.dynamic_slice_in_dim(packed_users, first_slot, 4, 0)
        result = prefix_attention(group_queries, group_users, prefix_keys, prefix_values)
        return lax.dynamic_update_slice_in_dim(buffer, result, first_slot, 0)

    packed_out = lax.fori_loop(
        0, needed, attend_group, jnp.zeros((total_slots, block_width, half_width), jnp.bfloat16)
    )
    inverse = jnp.argsort(packing)
    attended_slots = jnp.take(packed_out, inverse, axis=0)
    returned = lax.all_to_all(
        attended_slots.reshape(sources, per_source, block_width, half_width),
        "users",
        split_axis=0,
        concat_axis=0,
        tiled=True,
    )
    prefix_part = jnp.take(returned.reshape(slot_count, block_width * half_width), position, axis=0)
    prefix_part = prefix_part.reshape(row_count, heads_here, HEAD_DIM).astype(jnp.float32)
    query_heads = queries.astype(jnp.float32).reshape(row_count, heads_here, HEAD_DIM)
    self_keys = activated[1].reshape(row_count, heads_here, HEAD_DIM)
    self_values = activated[2].reshape(row_count, heads_here, HEAD_DIM)
    own_term = (
        jax.nn.silu(jnp.sum(query_heads * self_keys, axis=-1) * score_scale)[..., None]
        * self_values
    )
    attended = (prefix_part + own_term).reshape(row_count, half_width)
    totals = lax.psum((jnp.sum(attended, axis=1), jnp.sum(attended * attended, axis=1)), "heads")
    row_mean = totals[0] / HD
    row_var = totals[1] / HD - row_mean * row_mean
    gated = (
        (attended - row_mean[:, None])
        * lax.rsqrt(row_var + EPSILON)[:, None]
        * attn_gain.astype(jnp.float32)
        * activated[3]
    ).astype(jnp.bfloat16)
    partial_out = jnp.dot(
        gated,
        lax.all_gather(w_o, "routers", axis=1, tiled=True),
        preferred_element_type=jnp.float32,
    )
    mixed = lax.psum(partial_out, "heads")
    residual = flat_items.astype(jnp.float32) + mixed
    row_scale = lax.rsqrt(jnp.sum(residual * residual, axis=1) / D + EPSILON)
    normed = (residual * row_scale[:, None] * mlp_gain.astype(jnp.float32)).astype(jnp.bfloat16)
    hidden = jax.nn.silu(jnp.dot(normed, w_one, preferred_element_type=jnp.float32)).astype(
        jnp.bfloat16
    )
    block_scores = jnp.dot(hidden, w_two, preferred_element_type=jnp.float32).reshape(
        blocks, block_width
    )
    is_valid = lax.broadcasted_iota(jnp.int32, (blocks, block_width), 1) < block_fill[:, None]
    return jnp.where(is_valid, block_scores, jnp.zeros_like(block_scores))


def solution(mesh):
    placed = (
        P(("groups", "users", "routers"), None, None),
        P(("groups", "users", "routers"), None),
        P(("groups", "users", "routers")),
        P(("groups", "users", "routers")),
        P(("groups", "users"), None, "heads"),
        P(("groups", "users"), None, "heads"),
        P(None, "routers", "heads"),
        P("heads"),
        P("heads", "routers"),
        P(),
        P(),
        P(),
    )
    return jax.shard_map(
        local,
        mesh=mesh,
        in_specs=placed,
        out_specs=P(("groups", "users", "routers"), None),
        check_vma=False,
    )
```

profile of v0, /device:TPU:0, one launch (start us, length us, event | category | flops | bytes accessed | tf_op | source)
XLA Modules:
  0.0 166.5 jit_solution(10524344665358077682)
XLA Ops:
  6.5 4.2 %copy.36 = bf16[4,512,512]{1,2,0:T(8,128)(2,1)} copy(bf16[4,512,512]{2,1,0:T(8,128)(2,1)} %param.24) | data formatting | bytes 4194304 | tf_op args[6]
  10.8 0.0 all-gather.3.cloned.1.call-update
  10.8 0.6 copy-done.10
  11.4 0.2 convert_reduce_fusion
  11.6 0.0 copy-done.12
  11.6 0.1 select_reduce_fusion
  11.7 0.7 sub.21
  12.4 6.3 %all-to-all-start = ((s32[4,1,2]{2,1,0:T(1,128)}), s32[4,1,2]{2,1,0:T(1,128)S(1)}, u32[]{:S(2)}, u32[]{:S(2)}) async-start(s32[4,1,2]{2,1,0:T(1,128)} %bitcast.5), calls=%async_computation | async-start | bytes 4096 | tf_op jit(solution)/shard_map/all_to_all | solution.py:76
  18.7 0.7 all-gather.5.cloned.1.call-update
  19.4 4.8 %all-to-all-done = s32[4,1,2]{2,1,0:T(1,128)S(1)} async-done(((s32[4,1,2]{2,1,0:T(1,128)}), s32[4,1,2]{2,1,0:T(1,128)S(1)}, u32[]{:S(2)}, u32[]{:S(2)}) %all-to-all-start) | async-done | bytes 64 | tf_op jit(solution)/shard_map/all_to_all | solution.py:76
  24.2 0.5 broadcast.235
  24.7 1.3 fusion.40
  26.0 0.1 reshape.118
  26.1 1.0 sort.34
  27.1 43.4 %all-gather.3.cloned.1.call-done = bf16[4,1024,512]{1,2,0:T(8,128)(2,1)} async-done(((bf16[4,512,512]{1,2,0:T(8,128)(2,1)}), bf16[4,1024,512]{1,2,0:T(8,128)(2,1)}) %all-gather.3.cloned.1.call-update) | async-done | bytes 4194320 | tf_op jit(solution)/shard_map/all_gather | solution.py:55
  70.4 0.0 copy-done.7
  70.4 3.6 %bitcast_multiply_fusion = f32[4,256,512]{1,2,0:T(8,128)S(1)} fusion(bf16[4,1024,512]{1,2,0:T(8,128)(2,1)} %all-gather.3.cloned.1.call-done, bf16[256,1024,1]{1,0,2:T(8,128)(2,1)S(1)} %bitcast.106), kind=kOutput, calls=%fused_computation.28 | convolution fusion | flops 1075838976 | bytes 6815744 | tf_op jit(solution)/shard_map/rk,pkc->prc/dot_general | solution.py:52
  74.0 0.0 copy-start.5
  74.0 1.3 copy-done.5
  75.4 0.9 slice_multiply_fusion
  76.3 0.1 copy.37
  76.4 0.2 convert_element_type.76
  76.6 0.4 convolution_convert_fusion.1
  77.0 1.0 copy.43
  78.0 4.7 %all-to-all-start.1 = ((bf16[4,2,64,512]{3,2,1,0:T(8,128)(2,1)}), bf16[4,2,64,512]{3,2,1,0:T(8,128)(2,1)S(1)}, u32[]{:S(2)}, u32[]{:S(2)}) async-start(bf16[4,2,64,512]{3,2,1,0:T(8,128)(2,1)} %bitcast.27), calls=%async_computation.1 | async-start | bytes 1048576 | tf_op jit(solution)/shard_map/all_to_all | solution.py:75
  83.4 0.6 gather_fusion.2
  84.0 1.0 sort.35
  85.0 12.0 %all-to-all-done.1 = bf16[4,2,64,512]{3,2,1,0:T(8,128)(2,1)S(1)} async-done(((bf16[4,2,64,512]{3,2,1,0:T(8,128)(2,1)}), bf16[4,2,64,512]{3,2,1,0:T(8,128)(2,1)S(1)}, u32[]{:S(2)}, u32[]{:S(2)}) %all-to-all-start.1) | async-done | bytes 524320 | tf_op jit(solution)/shard_map/all_to_all | solution.py:75
  97.0 0.6 gather_fusion.4
  97.6 0.9 broadcast_select_fusion.1
  98.6 0.9 broadcast_in_dim.66
  99.4 6.1 %while.10 = (s32[]{:T(128)}, bf16[8,64,512]{2,1,0:T(8,128)(2,1)}, s32[]{:T(128)}, s32[8]{0:T(128)S(1)}, bf16[2,256,512]{2,1,0:T(8,128)(2,1)S(1)}, /*index=5*/bf1...) while((s32[]{:T(128)}, bf16[8,64,512]{2,1,0:T(8,128)(2,1)}, ...), condition=%wide.region_5.8_spmd, body=%wide.region_4.7_spmd.sunk | while | flops 136971280 | bytes 13635875 | solution.py:94
  99.4 0.1 broadcast_compare_fusion.2
  99.5 0.6 gather_fusion
  100.1 0.6 gather_fusion.1
  100.7 1.5 select_bitcast_fusion.3
  102.3 2.5 %fusion.55 = bf16[4,4,8,8,128]{4,3,2,1,0:T(8,128)(2,1)S(1)} fusion(bf16[4,32,4,8,128]{4,3,2,1,0:T(8,128)(2,1)} %get-tuple-element.135, bf16[4,32,4,8,128]{4,3,2,1,0:T(8,128)(2,1)} %get-tuple-element.136, bf16[8,64,512]{2,1,0:T(8,128)(2,1)} %get-tuple-element.164, s32[]{:T(128)S(6)} %select_n.93), kind=kOutput, calls=%fused_computation.8.clone.1 | convolution fusion | flops 135921664 | bytes 2621444 | tf_op jit(solution)/shard_map/while/body/ghqk,gkhd->gqhd/dot_general | solution.py:26
  104.8 0.7 bitcast_dynamic-update-slice_fusion.2
  105.5 1.7 %gather_fusion.5 = bf16[8,64,512]{2,1,0:T(8,128)(2,1)S(1)} fusion(bf16[8,64,512]{2,1,0:T(8,128)(2,1)} %get-tuple-element.174, s32[1024]{0:T(1024)S(1)} %pad_clamp_fusion.2), kind=kCustom, calls=%fused_computation.2.clone | custom fusion | bytes 1048608 | tf_op jit(solution)/shard_map/jit(_take)/gather | solution.py:98
  107.2 0.9 broadcast_select_fusion
  108.1 3.5 %all-to-all-start.2 = ((bf16[4,2,64,512]{3,2,1,0:T(8,128)(2,1)}), bf16[4,2,64,512]{3,2,1,0:T(8,128)(2,1)S(1)}, u32[]{:S(2)}, u32[]{:S(2)}) async-start(bf16[4,2,64,512]{3,2,1,0:T(8,128)(2,1)} %bitcast.9), calls=%async_computation.2 | async-start | bytes 1048576 | tf_op jit(solution)/shard_map/all_to_all | solution.py:99
  111.6 0.0 all-reduce.3.cloned.1.call-start
  111.7 0.1 broadcast_in_dim.63
  111.8 0.1 broadcast_in_dim.64
  111.9 13.7 %all-to-all-done.2 = bf16[4,2,64,512]{3,2,1,0:T(8,128)(2,1)S(1)} async-done(((bf16[4,2,64,512]{3,2,1,0:T(8,128)(2,1)}), bf16[4,2,64,512]{3,2,1,0:T(8,128)(2,1)S(1)}, u32[]{:S(2)}, u32[]{:S(2)}) %all-to-all-start.2) | async-done | bytes 524320 | tf_op jit(solution)/shard_map/all_to_all | solution.py:99
  125.6 0.3 copy.44
  125.9 0.0 copy-start.6
  125.9 0.8 gather_fusion.3
  126.7 0.2 gather.18
  126.9 0.1 copy.38
  127.1 0.5 copy-done.6
  127.5 0.1 fusion.39
  127.7 2.5 %all-reduce = (f32[256]{0:T(256)S(1)}, f32[256]{0:T(256)S(1)}) all-reduce(f32[256]{0:T(256)S(1)} %get-tuple-element.51, f32[256]{0:T(256)S(1)} %get-tuple-element.50), channel_id=1, replica_groups=mesh['groups'=2,'users'=4,'routers'=2,'heads'=2] {'heads'}, use_global_device_ids=true, to_apply=%region_11.14 | all-reduce | flops 512 | bytes 4096 | tf_op jit(solution)/shard_map/psum | solution.py:116
  130.1 0.0 all-gather.5.cloned.1.call-done
  130.2 0.0 copy-start.9
  130.2 0.0 copy-start.14
  130.2 2.8 %fusion.27 = f32[256,1024]{1,0:T(8,128)} fusion(bf16[512,1024]{1,0:T(8,128)(2,1)} %all-gather.5.cloned.1.call-done, f32[4,256,512]{1,2,0:T(8,128)S(1)} %copy-done.6, f32[256,512]{0,1:T(8,128)S(1)} %get-tuple-element.72, f32[512]{0:T(512)S(1)} %convert_element_type.80, f32[256]{0:T(256)S(1)} %get-tuple-element.82, f32[256]{0:T(256)S(1)} %get-tuple-element.81), kind=kOutput, calls=%fused_computation.50 | convolution fusion | flops 269090816 | bytes 3149824 | tf_op jit(solution)/shard_map/dot_general | solution.py:125
  133.0 0.0 all-reduce.3.cloned.1.call-update
  133.0 0.0 copy-start.13
  133.1 22.9 %all-reduce.3.cloned.1.call-done = f32[256,1024]{1,0:T(8,128)} async-done(((f32[256,1024]{1,0:T(8,128)}), f32[256,1024]{1,0:T(8,128)}) %all-reduce.3.cloned.1.call-update) | async-done | bytes 1048592 | tf_op jit(solution)/shard_map/psum | solution.py:130
  155.9 1.6 multiply_reduce_fusion
  157.5 1.7 %fusion.29 = f32[1,256]{1,0:T(1,128)S(1)} fusion(bf16[256,1]{0,1:T(2,128)(2,1)S(1)} %reshape.186, bf16[1024,256]{1,0:T(8,128)(2,1)S(1)} %copy-done, f32[256,1024]{1,0:T(8,128)} %all-reduce.3.cloned.1.call-done, bf16[256,1024]{1,0:T(8,128)(2,1)S(1)} %bitcast.107, f32[1024]{0:T(1024)S(1)} %convert_element_type.82, f32[256]{0:T(256)S(1)} %add_rsqrt_fusion), kind=kOutput, calls=%fused_computation.52 | convolution fusion | flops 135987200 | bytes 2103808 | tf_op jit(solution)/shard_map/dot_general | solution.py:137
  159.2 0.1 reshape.123
  159.3 0.7 fusion.35
  (43 shorter events, 0.2 us)
Async XLA Ops:
  6.5 151.0 %copy-start = (bf16[1024,256]{1,0:T(8,128)(2,1)S(1)}, bf16[1024,256]{1,0:T(8,128)(2,1)}, u32[]{:S(2)}) copy-start(bf16[1024,256]{1,0:T(8,128)(2,1)} %param.28) | copy-start | bytes 1572868
  6.5 63.9 %all-gather.3.cloned.1.call-start = ((), (), s32[]{:S(2)}) async-start(), calls=%async_computation.3 | async-start | bytes 6291456 | tf_op jit(solution)/shard_map/all_gather | solution.py:55
  10.7 0.7 copy-start.10
  10.7 0.8 copy-start.12
  10.8 59.7 %copy-start.7 = (bf16[4,64,1024]{2,1,0:T(8,128)(2,1)S(1)}, bf16[4,64,1024]{2,1,0:T(8,128)(2,1)}, u32[]{:S(2)}) copy-start(bf16[4,64,1024]{2,1,0:T(8,128)(2,1)} %param.18) | copy-start | bytes 1572868
  12.4 11.8 %all-to-all-start = ((s32[4,1,2]{2,1,0:T(1,128)}), s32[4,1,2]{2,1,0:T(1,128)S(1)}, u32[]{:S(2)}, u32[]{:S(2)}) async-start(s32[4,1,2]{2,1,0:T(1,128)} %bitcast.5), calls=%async_computation | async-start | bytes 4096 | tf_op jit(solution)/shard_map/all_to_all | solution.py:76
  18.7 111.4 %all-gather.5.cloned.1.call-start = ((), (), s32[]{:S(2)}) async-start(), calls=%async_computation.4 | async-start | bytes 1572864 | tf_op jit(solution)/shard_map/all_gather | solution.py:127
  74.0 1.4 copy-start.5
  78.0 21.4 %copy-start.1 = (bf16[2,256,512]{2,1,0:T(8,128)(2,1)S(1)}, bf16[2,256,512]{2,1,0:T(8,128)(2,1)}, u32[]{:S(2)}) copy-start(bf16[2,256,512]{2,1,0:T(8,128)(2,1)} %param.23) | copy-start | bytes 1572868
  78.0 21.4 %copy-start.2 = (bf16[2,256,512]{2,1,0:T(8,128)(2,1)S(1)}, bf16[2,256,512]{2,1,0:T(8,128)(2,1)}, u32[]{:S(2)}) copy-start(bf16[2,256,512]{2,1,0:T(8,128)(2,1)} %param.22) | copy-start | bytes 1572868
  78.0 19.1 %all-to-all-start.1 = ((bf16[4,2,64,512]{3,2,1,0:T(8,128)(2,1)}), bf16[4,2,64,512]{3,2,1,0:T(8,128)(2,1)S(1)}, u32[]{:S(2)}, u32[]{:S(2)}) async-start(bf16[4,2,64,512]{3,2,1,0:T(8,128)(2,1)} %bitcast.27), calls=%async_computation.1 | async-start | bytes 1048576 | tf_op jit(solution)/shard_map/all_to_all | solution.py:75
  102.3 3.2 %copy-start.3 = (bf16[2,256,512]{2,1,0:T(8,128)(2,1)S(1)}, bf16[2,256,512]{2,1,0:T(8,128)(2,1)}, u32[]{:S(2)}) copy-start(bf16[2,256,512]{2,1,0:T(8,128)(2,1)} %get-tuple-element.184) | copy-start | bytes 1572868 | tf_op jit(solution)/shard_map/while
  105.5 6.3 %copy-start.11 = (bf16[512]{0:T(512)(128)(2,1)S(1)}, bf16[512]{0:T(512)(128)(2,1)}, u32[]{:S(2)}) copy-start(bf16[512]{0:T(512)(128)(2,1)} %param.25) | copy-start | bytes 3076
  105.5 6.3 %copy-start.4 = (f32[1,256,512]{1,2,0:T(8,128)S(1)}, f32[1,256,512]{1,2,0:T(8,128)}, u32[]{:S(2)}) copy-start(f32[1,256,512]{1,2,0:T(8,128)} %get-tuple-element.77) | copy-start | bytes 1572868
  108.1 17.5 %all-to-all-start.2 = ((bf16[4,2,64,512]{3,2,1,0:T(8,128)(2,1)}), bf16[4,2,64,512]{3,2,1,0:T(8,128)(2,1)S(1)}, u32[]{:S(2)}, u32[]{:S(2)}) async-start(bf16[4,2,64,512]{3,2,1,0:T(8,128)(2,1)} %bitcast.9), calls=%async_computation.2 | async-start | bytes 1048576 | tf_op jit(solution)/shard_map/all_to_all | solution.py:99
  111.6 44.3 %all-reduce.3.cloned.1.call-start = ((), (), s32[]{:S(2)}) async-start(), calls=%async_computation.5 | async-start | bytes 2097152 | tf_op jit(solution)/shard_map/psum | solution.py:130
  125.9 1.6 copy-start.6
  130.2 2.8 %copy-start.9 = (bf16[1024]{0:T(1024)(128)(2,1)S(1)}, bf16[1024]{0:T(1024)(128)(2,1)}, u32[]{:S(2)}) copy-start(bf16[1024]{0:T(1024)(128)(2,1)} %param.27) | copy-start | bytes 6148
  130.2 2.9 %copy-start.14 = (bf16[256]{0:T(256)(128)(2,1)S(1)}, bf16[256]{0:T(256)(128)(2,1)}, u32[]{:S(2)}) copy-start(bf16[256]{0:T(256)(128)(2,1)} %param.29) | copy-start | bytes 1540
  133.0 24.5 %copy-start.8 = (bf16[4,64,1024]{2,1,0:T(8,128)(2,1)S(1)}, bf16[4,64,1024]{2,1,0:T(8,128)(2,1)}, u32[]{:S(2)}) copy-start(bf16[4,64,1024]{2,1,0:T(8,128)(2,1)} %param.18) | copy-start | bytes 1572868
  133.0 26.3 %copy-start.13 = (s32[4]{0:T(128)S(1)}, s32[4]{0:T(128)}, u32[]{:S(2)}) copy-start(s32[4]{0:T(128)} %param.21) | copy-start | bytes 52
Sparse Core Ops, SparseCore 0:
  10.9 59.4 all-gather.2
  72.0 21.2 all-gather.4
  133.1 22.7 all-reduce.2
where the time goes:
time: 167 us; the launch traced here: 166 us
  waiting for transfers between devices  97.4 us (58%)
  local copies, waits for them, and re-layouts  16.6 us (10%)
  starting transfers between devices  14.6 us (9%)
  between operations  14 us (8%)
  matrix products  11 us (7%)
  other arithmetic  10.4 us (6%)
  blocking collectives  2.46 us (1%)
    all_gather x1, waiting for transfers between devices, local(): lax.all_gather(w_in, 'routers', axis=1, tiled=True)  43.4 us
    psum x1, waiting for transfers between devices, local(): mixed = lax.psum(partial_out, 'heads')  22.9 us
    all_to_all x1, waiting for transfers between devices, local(): lax.all_to_all(attended_slots.reshape(sources, per_source, block_width, h...  13.7 us
    all_to_all x1, waiting for transfers between devices, local(): lax.all_to_all(outgoing, 'users', split_axis=0, concat_axis=0, tiled=True)  12 us
    unnamed x32, local copies, waits for them, and re-layouts  7.95 us
    all_to_all x1, starting transfers between devices, local(): lax.all_to_all(slot_user, 'users', split_axis=0, concat_axis=0, tiled=True)  6.35 us
    all_to_all x1, waiting for transfers between devices, local(): lax.all_to_all(slot_user, 'users', split_axis=0, concat_axis=0, tiled=True)  4.76 us
    all_to_all x1, starting transfers between devices, local(): lax.all_to_all(outgoing, 'users', split_axis=0, concat_axis=0, tiled=True)  4.73 us
  transfers between devices with their start and end apart: 6, of which 5 were waited for; matrix products, arithmetic and copies ran while one was open for 15% of the time, Pallas kernels for 0%

commit v1 on v0

--- a/solution.py
+++ b/solution.py
@@ -127,7 +127,8 @@
         lax.all_gather(w_o, "routers", axis=1, tiled=True),
         preferred_element_type=jnp.float32,
     )
-    mixed = lax.psum(partial_out, "heads")
+    parts = lax.all_gather(partial_out, "heads", axis=0, tiled=False)
+    mixed = parts.sum(axis=0)
     residual = flat_items.astype(jnp.float32) + mixed
     row_scale = lax.rsqrt(jnp.sum(residual * residual, axis=1) / D + EPSILON)
     normed = (residual * row_scale[:, None] * mlp_gain.astype(jnp.float32)).astype(jnp.bfloat16)

time: 167 us -> 158 us (0.946)
  waiting for transfers between devices: 97.4 us -> 88.6 us
    psum x1 -> x0, waiting for transfers between devices: 22.9 us -> none  [local(): mixed = lax.psum(partial_out, 'heads')]
    all_gather x0 -> x1, waiting for transfers between devices: none -> 14 us  [local(): parts = lax.all_gather(partial_out, 'heads', axis=0, tiled=False)]
    reduce_sum x0 -> x1, other arithmetic: none -> 1.85 us  [local(): mixed = parts.sum(axis=0)]
  transfers between devices with their start and end apart: 6 -> 6, of which waited for: 5 -> 5; matrix products, arithmetic and copies ran while one was open for 15% -> 16% of each run, Pallas kernels for 0% -> 0%
where the time goes in v1:
time: 158 us; the launch traced here: 157 us
  waiting for transfers between devices  88.6 us (56%)
  local copies, waits for them, and re-layouts  16.7 us (11%)
  starting transfers between devices  14.6 us (9%)
  between operations  14 us (9%)
  other arithmetic  10.9 us (7%)
  matrix products  9.75 us (6%)
  blocking collectives  2.46 us (2%)
    all_gather x1, waiting for transfers between devices, local(): lax.all_gather(w_in, 'routers', axis=1, tiled=True)  43.4 us
    all_gather x1, waiting for transfers between devices, local(): parts = lax.all_gather(partial_out, 'heads', axis=0, tiled=False)  14 us
    all_to_all x1, waiting for transfers between devices, local(): lax.all_to_all(attended_slots.reshape(sources, per_source, block_width, h...  13.7 us
    all_to_all x1, waiting for transfers between devices, local(): lax.all_to_all(outgoing, 'users', split_axis=0, concat_axis=0, tiled=True)  12 us
    unnamed x32, local copies, waits for them, and re-layouts  7.95 us
    all_to_all x1, starting transfers between devices, local(): lax.all_to_all(slot_user, 'users', split_axis=0, concat_axis=0, tiled=True)  6.35 us
    all_to_all x1, waiting for transfers between devices, local(): lax.all_to_all(slot_user, 'users', split_axis=0, concat_axis=0, tiled=True)  4.76 us
    all_to_all x1, starting transfers between devices, local(): lax.all_to_all(outgoing, 'users', split_axis=0, concat_axis=0, tiled=True)  4.73 us
  transfers between devices with their start and end apart: 6, of which 5 were waited for; matrix products, arithmetic and copies ran while one was open for 16% of the time, Pallas kernels for 0%

profile of v1, /device:TPU:0, one launch (start us, length us, event | category | flops | bytes accessed | tf_op | source)
XLA Modules:
  0.0 157.0 jit_solution(7574882432108518667)
XLA Ops:
  6.5 4.2 %copy.36 = bf16[4,512,512]{1,2,0:T(8,128)(2,1)} copy(bf16[4,512,512]{2,1,0:T(8,128)(2,1)} %param.24) | data formatting | bytes 4194304 | tf_op args[6]
  10.8 0.0 all-gather.5.cloned.1.call-update
  10.8 0.6 copy-done.10
  11.4 0.2 convert_reduce_fusion
  11.6 0.0 copy-done.12
  11.6 0.1 select_reduce_fusion
  11.7 0.7 sub.21
  12.4 6.3 %all-to-all-start = ((s32[4,1,2]{2,1,0:T(1,128)}), s32[4,1,2]{2,1,0:T(1,128)S(1)}, u32[]{:S(2)}, u32[]{:S(2)}) async-start(s32[4,1,2]{2,1,0:T(1,128)} %bitcast.5), calls=%async_computation | async-start | bytes 4096 | tf_op jit(solution)/shard_map/all_to_all | solution.py:76
  18.7 0.7 all-gather.7.cloned.1.call-update
  19.4 4.8 %all-to-all-done = s32[4,1,2]{2,1,0:T(1,128)S(1)} async-done(((s32[4,1,2]{2,1,0:T(1,128)}), s32[4,1,2]{2,1,0:T(1,128)S(1)}, u32[]{:S(2)}, u32[]{:S(2)}) %all-to-all-start) | async-done | bytes 64 | tf_op jit(solution)/shard_map/all_to_all | solution.py:76
  24.2 0.5 broadcast.245
  24.7 1.3 fusion.40
  26.0 0.1 reshape.128
  26.1 1.0 sort.34
  27.1 43.4 %all-gather.5.cloned.1.call-done = bf16[4,1024,512]{1,2,0:T(8,128)(2,1)} async-done(((bf16[4,512,512]{1,2,0:T(8,128)(2,1)}), bf16[4,1024,512]{1,2,0:T(8,128)(2,1)}) %all-gather.5.cloned.1.call-update) | async-done | bytes 4194320 | tf_op jit(solution)/shard_map/all_gather | solution.py:55
  70.4 0.0 copy-done.7
  70.4 3.6 %bitcast_multiply_fusion = f32[4,256,512]{1,2,0:T(8,128)S(1)} fusion(bf16[4,1024,512]{1,2,0:T(8,128)(2,1)} %all-gather.5.cloned.1.call-done, bf16[256,1024,1]{1,0,2:T(8,128)(2,1)S(1)} %bitcast.109), kind=kOutput, calls=%fused_computation.28 | convolution fusion | flops 1075838976 | bytes 6815744 | tf_op jit(solution)/shard_map/rk,pkc->prc/dot_general | solution.py:52
  74.0 1.3 copy-done.5
  75.4 0.9 slice_multiply_fusion
  76.3 0.1 copy.37
  76.4 0.2 convert_element_type.79
  76.6 0.4 convolution_convert_fusion.1
  77.0 1.0 copy.43
  78.0 4.7 %all-to-all-start.1 = ((bf16[4,2,64,512]{3,2,1,0:T(8,128)(2,1)}), bf16[4,2,64,512]{3,2,1,0:T(8,128)(2,1)S(1)}, u32[]{:S(2)}, u32[]{:S(2)}) async-start(bf16[4,2,64,512]{3,2,1,0:T(8,128)(2,1)} %bitcast.29), calls=%async_computation.1 | async-start | bytes 1048576 | tf_op jit(solution)/shard_map/all_to_all | solution.py:75
  83.4 0.6 gather_fusion.2
  84.0 1.0 sort.35
  85.0 12.0 %all-to-all-done.1 = bf16[4,2,64,512]{3,2,1,0:T(8,128)(2,1)S(1)} async-done(((bf16[4,2,64,512]{3,2,1,0:T(8,128)(2,1)}), bf16[4,2,64,512]{3,2,1,0:T(8,128)(2,1)S(1)}, u32[]{:S(2)}, u32[]{:S(2)}) %all-to-all-start.1) | async-done | bytes 524320 | tf_op jit(solution)/shard_map/all_to_all | solution.py:75
  97.0 0.6 gather_fusion.4
  97.6 0.9 broadcast_select_fusion.1
  98.6 0.9 broadcast_in_dim.66
  99.4 6.1 %while.10 = (s32[]{:T(128)}, bf16[8,64,512]{2,1,0:T(8,128)(2,1)}, s32[]{:T(128)}, s32[8]{0:T(128)S(1)}, bf16[2,256,512]{2,1,0:T(8,128)(2,1)S(1)}, /*index=5*/bf1...) while((s32[]{:T(128)}, bf16[8,64,512]{2,1,0:T(8,128)(2,1)}, ...), condition=%wide.region_5.8_spmd, body=%wide.region_4.7_spmd.sunk | while | flops 136971280 | bytes 13635875 | solution.py:94
  99.4 0.1 broadcast_compare_fusion.2
  99.5 0.6 gather_fusion
  100.1 0.6 gather_fusion.1
  100.7 1.5 select_bitcast_fusion.3
  102.3 2.5 %fusion.55 = bf16[4,4,8,8,128]{4,3,2,1,0:T(8,128)(2,1)S(1)} fusion(bf16[4,32,4,8,128]{4,3,2,1,0:T(8,128)(2,1)} %get-tuple-element.135, bf16[4,32,4,8,128]{4,3,2,1,0:T(8,128)(2,1)} %get-tuple-element.136, bf16[8,64,512]{2,1,0:T(8,128)(2,1)} %get-tuple-element.164, s32[]{:T(128)S(6)} %select_n.93), kind=kOutput, calls=%fused_computation.8.clone.1 | convolution fusion | flops 135921664 | bytes 2621444 | tf_op jit(solution)/shard_map/while/body/ghqk,gkhd->gqhd/dot_general | solution.py:26
  104.8 0.7 bitcast_dynamic-update-slice_fusion.2
  105.5 1.7 %gather_fusion.5 = bf16[8,64,512]{2,1,0:T(8,128)(2,1)S(1)} fusion(bf16[8,64,512]{2,1,0:T(8,128)(2,1)} %get-tuple-element.174, s32[1024]{0:T(1024)S(1)} %pad_clamp_fusion.2), kind=kCustom, calls=%fused_computation.2.clone | custom fusion | bytes 1048608 | tf_op jit(solution)/shard_map/jit(_take)/gather | solution.py:98
  107.2 0.9 broadcast_select_fusion
  108.1 3.5 %all-to-all-start.2 = ((bf16[4,2,64,512]{3,2,1,0:T(8,128)(2,1)}), bf16[4,2,64,512]{3,2,1,0:T(8,128)(2,1)S(1)}, u32[]{:S(2)}, u32[]{:S(2)}) async-start(bf16[4,2,64,512]{3,2,1,0:T(8,128)(2,1)} %bitcast.9), calls=%async_computation.2 | async-start | bytes 1048576 | tf_op jit(solution)/shard_map/all_to_all | solution.py:99
  111.6 0.0 all-gather.9.cloned.1.call-start
  111.7 0.1 broadcast_in_dim.63
  111.8 0.1 broadcast_in_dim.64
  111.9 13.7 %all-to-all-done.2 = bf16[4,2,64,512]{3,2,1,0:T(8,128)(2,1)S(1)} async-done(((bf16[4,2,64,512]{3,2,1,0:T(8,128)(2,1)}), bf16[4,2,64,512]{3,2,1,0:T(8,128)(2,1)S(1)}, u32[]{:S(2)}, u32[]{:S(2)}) %all-to-all-start.2) | async-done | bytes 524320 | tf_op jit(solution)/shard_map/all_to_all | solution.py:99
  125.6 0.3 copy.44
  125.9 0.8 gather_fusion.3
  126.7 0.2 gather.18
  126.9 0.1 copy.38
  127.1 0.5 copy-done.6
  127.5 0.1 fusion.39
  127.7 2.5 %all-reduce = (f32[256]{0:T(256)S(1)}, f32[256]{0:T(256)S(1)}) all-reduce(f32[256]{0:T(256)S(1)} %get-tuple-element.51, f32[256]{0:T(256)S(1)} %get-tuple-element.50), channel_id=1, replica_groups=mesh['groups'=2,'users'=4,'routers'=2,'heads'=2] {'heads'}, use_global_device_ids=true, to_apply=%region_11.14 | all-reduce | flops 512 | bytes 4096 | tf_op jit(solution)/shard_map/psum | solution.py:116
  130.1 0.0 all-gather.7.cloned.1.call-done
  130.2 0.0 copy-start.9
  130.2 0.0 copy-start.14
  130.2 2.8 %fusion.27 = f32[256,1024]{1,0:T(8,128)} fusion(bf16[512,1024]{1,0:T(8,128)(2,1)} %all-gather.7.cloned.1.call-done, f32[4,256,512]{1,2,0:T(8,128)S(1)} %copy-done.6, f32[256,512]{0,1:T(8,128)S(1)} %get-tuple-element.72, f32[512]{0:T(512)S(1)} %convert_element_type.83, f32[256]{0:T(256)S(1)} %get-tuple-element.82, f32[256]{0:T(256)S(1)} %get-tuple-element.81), kind=kOutput, calls=%fused_computation.49 | convolution fusion | flops 269090816 | bytes 3149824 | tf_op jit(solution)/shard_map/dot_general | solution.py:125
  133.0 0.0 all-gather.9.cloned.1.call-update
  133.0 14.0 %all-gather.9.cloned.1.call-done = f32[512,1024]{1,0:T(8,128)} async-done(((f32[256,1024]{1,0:T(8,128)}), f32[512,1024]{1,0:T(8,128)}) %all-gather.9.cloned.1.call-update) | async-done | bytes 2097168 | tf_op jit(solution)/shard_map/all_gather | solution.py:130
  147.0 1.8 %reduce_sum.83 = f32[256,1024]{1,0:T(8,128)S(1)} reduce(f32[2,256,1024]{2,1,0:T(8,128)} %bitcast.105, f32[]{:T(128)} %constant.102.clone.1), dimensions={0}, to_apply=%region_12.15 | reduce | flops 262144 | bytes 3145732 | tf_op jit(solution)/shard_map/reduce_sum | solution.py:131
  148.9 0.0 copy-start.13
  148.9 0.2 multiply_reduce_fusion
  149.1 0.1 rsqrt.15
  149.2 0.5 fusion.29
  149.7 0.1 reshape.133
  149.8 0.7 fusion.35
  (45 shorter events, 0.2 us)
Async XLA Ops:
  6.5 142.7 %copy-start = (bf16[1024,256]{1,0:T(8,128)(2,1)S(1)}, bf16[1024,256]{1,0:T(8,128)(2,1)}, u32[]{:S(2)}) copy-start(bf16[1024,256]{1,0:T(8,128)(2,1)} %param.28) | copy-start | bytes 1572868
  6.5 63.9 %all-gather.5.cloned.1.call-start = ((), (), s32[]{:S(2)}) async-start(), calls=%async_computation.3 | async-start | bytes 6291456 | tf_op jit(solution)/shard_map/all_gather | solution.py:55
  10.7 0.7 copy-start.10
  10.7 0.8 copy-start.12
  10.8 59.7 %copy-start.7 = (bf16[4,64,1024]{2,1,0:T(8,128)(2,1)S(1)}, bf16[4,64,1024]{2,1,0:T(8,128)(2,1)}, u32[]{:S(2)}) copy-start(bf16[4,64,1024]{2,1,0:T(8,128)(2,1)} %param.18) | copy-start | bytes 1572868
  12.4 11.8 %all-to-all-start = ((s32[4,1,2]{2,1,0:T(1,128)}), s32[4,1,2]{2,1,0:T(1,128)S(1)}, u32[]{:S(2)}, u32[]{:S(2)}) async-start(s32[4,1,2]{2,1,0:T(1,128)} %bitcast.5), calls=%async_computation | async-start | bytes 4096 | tf_op jit(solution)/shard_map/all_to_all | solution.py:76
  18.7 111.4 %all-gather.7.cloned.1.call-start = ((), (), s32[]{:S(2)}) async-start(), calls=%async_computation.4 | async-start | bytes 1572864 | tf_op jit(solution)/shard_map/all_gather | solution.py:127
  74.0 1.4 copy-start.5
  78.0 21.4 %copy-start.1 = (bf16[2,256,512]{2,1,0:T(8,128)(2,1)S(1)}, bf16[2,256,512]{2,1,0:T(8,128)(2,1)}, u32[]{:S(2)}) copy-start(bf16[2,256,512]{2,1,0:T(8,128)(2,1)} %param.23) | copy-start | bytes 1572868
  78.0 21.4 %copy-start.2 = (bf16[2,256,512]{2,1,0:T(8,128)(2,1)S(1)}, bf16[2,256,512]{2,1,0:T(8,128)(2,1)}, u32[]{:S(2)}) copy-start(bf16[2,256,512]{2,1,0:T(8,128)(2,1)} %param.22) | copy-start | bytes 1572868
  78.0 19.1 %all-to-all-start.1 = ((bf16[4,2,64,512]{3,2,1,0:T(8,128)(2,1)}), bf16[4,2,64,512]{3,2,1,0:T(8,128)(2,1)S(1)}, u32[]{:S(2)}, u32[]{:S(2)}) async-start(bf16[4,2,64,512]{3,2,1,0:T(8,128)(2,1)} %bitcast.29), calls=%async_computation.1 | async-start | bytes 1048576 | tf_op jit(solution)/shard_map/all_to_all | solution.py:75
  102.3 3.2 %copy-start.3 = (bf16[2,256,512]{2,1,0:T(8,128)(2,1)S(1)}, bf16[2,256,512]{2,1,0:T(8,128)(2,1)}, u32[]{:S(2)}) copy-start(bf16[2,256,512]{2,1,0:T(8,128)(2,1)} %get-tuple-element.184) | copy-start | bytes 1572868 | tf_op jit(solution)/shard_map/while
  105.5 6.3 %copy-start.11 = (bf16[512]{0:T(512)(128)(2,1)S(1)}, bf16[512]{0:T(512)(128)(2,1)}, u32[]{:S(2)}) copy-start(bf16[512]{0:T(512)(128)(2,1)} %param.25) | copy-start | bytes 3076
  105.5 6.3 %copy-start.4 = (f32[1,256,512]{1,2,0:T(8,128)S(1)}, f32[1,256,512]{1,2,0:T(8,128)}, u32[]{:S(2)}) copy-start(f32[1,256,512]{1,2,0:T(8,128)} %get-tuple-element.77) | copy-start | bytes 1572868
  108.1 17.5 %all-to-all-start.2 = ((bf16[4,2,64,512]{3,2,1,0:T(8,128)(2,1)}), bf16[4,2,64,512]{3,2,1,0:T(8,128)(2,1)S(1)}, u32[]{:S(2)}, u32[]{:S(2)}) async-start(bf16[4,2,64,512]{3,2,1,0:T(8,128)(2,1)} %bitcast.9), calls=%async_computation.2 | async-start | bytes 1048576 | tf_op jit(solution)/shard_map/all_to_all | solution.py:99
  111.6 35.4 %all-gather.9.cloned.1.call-start = ((), (), s32[]{:S(2)}) async-start(), calls=%async_computation.5 | async-start | bytes 3145728 | tf_op jit(solution)/shard_map/all_gather | solution.py:130
  125.9 1.6 %copy-start.6 = (f32[4,256,512]{1,2,0:T(8,128)S(1)}, f32[4,256,512]{1,2,0:T(8,128)}, u32[]{:S(2)}) copy-start(f32[4,256,512]{1,2,0:T(8,128)} %copy-done.5) | copy-start | bytes 6291460
  130.2 2.8 %copy-start.9 = (bf16[1024]{0:T(1024)(128)(2,1)S(1)}, bf16[1024]{0:T(1024)(128)(2,1)}, u32[]{:S(2)}) copy-start(bf16[1024]{0:T(1024)(128)(2,1)} %param.27) | copy-start | bytes 6148
  130.2 2.8 %copy-start.14 = (bf16[256]{0:T(256)(128)(2,1)S(1)}, bf16[256]{0:T(256)(128)(2,1)}, u32[]{:S(2)}) copy-start(bf16[256]{0:T(256)(128)(2,1)} %param.29) | copy-start | bytes 1540
  133.0 15.9 %copy-start.8 = (bf16[4,64,1024]{2,1,0:T(8,128)(2,1)S(1)}, bf16[4,64,1024]{2,1,0:T(8,128)(2,1)}, u32[]{:S(2)}) copy-start(bf16[4,64,1024]{2,1,0:T(8,128)(2,1)} %param.18) | copy-start | bytes 1572868
  148.9 0.9 copy-start.13
Sparse Core Ops, SparseCore 0:
  10.9 59.4 all-gather.4
  72.0 21.2 all-gather.6
  133.1 13.8 all-gather.8
